TPU v7x, 256 devices: a whole 4x4x8 slice. The times are simulated.
256 devices in a mesh: row: 8 (over z_hi, x), col: 32 (over z_lo, y, core).
Axes of the slice: x: 4, y: 4, z: 8 (z_hi: 2, z_lo: 4; z = z_hi * 4 + z_lo), core: 2. Of those that a mesh axis runs over, the one named last changes fastest.
Arguments:
- matrix: bfloat16 [3072, 262144], P('row', 'col'), may hold values from -0.01171875 to 0.01171875
- probes: bfloat16 [262144, 128], P('col'), may hold values from -6 to 6
Outputs:
- krylov: bfloat16 [2, 262144, 128], P(None, 'col')
All inputs are finite; a program needn't handle non-finite values.
Results may differ from a plain program's by a relative error of at most 0.0054.
Values may be sent and summed in bfloat16 or wider, within the bound.
A program may use at most 64 MiB of HBM per device.

v0:
```python
import math

import jax
import jax.numpy as jnp
from jax import lax
from jax.sharding import Mesh
from jax.sharding import PartitionSpec as P

ITERS = 2
ROW = ("row_0", "row_1")


def cut_along(shard, dim, length):
    before, after = (shard.shape[:dim], shard.shape[dim + 1 :])
    return jnp.moveaxis(shard.reshape(*before, length, -1, *after), dim, 0)


def summed_on_arrival(shard, axis, dim):
    blocks = cut_along(shard, dim, lax.axis_size(axis))
    arrived = lax.all_to_all(blocks, axis, split_axis=0, concat_axis=0, tiled=True)
    return arrived.sum(axis=0)


def joined_along(blocks, dim):
    blocks = jnp.moveaxis(blocks, 0, dim)
    dims = blocks.shape
    return blocks.reshape(*dims[:dim], dims[dim] * dims[dim + 1], *dims[dim + 2 :])


def copy_for_each(shard, axis):
    length = lax.axis_size(axis)
    return lax.all_to_all(
        jnp.broadcast_to(shard[None], (length, *shard.shape)), axis, 0, 0, tiled=True
    )


def collect(shard, axis, dim):
    return joined_along(copy_for_each(shard, axis), dim)


def sum_in_order(blocks, axes, sequence):
    inside = blocks.shape[1:]
    blocks = blocks.reshape(*(lax.axis_size(a) for a in axes), *inside)
    blocks = jnp.moveaxis(blocks, sequence, range(len(axes))).reshape(-1, *inside)
    for k in sequence:
        blocks = lax.psum_scatter(blocks, axes[k], scatter_dimension=0, tiled=True)
    return blocks[0]


def summed_rows(shard, axes, sequence, dim):
    length = lax.axis_size(axes)
    return sum_in_order(cut_along(shard, dim, length), axes, sequence)


def body(matrix, probes):
    m_total = matrix.shape[0] * lax.axis_size(ROW)
    n_total = matrix.shape[1] * lax.axis_size("col")
    stretch = math.sqrt(n_total / m_total)
    current = probes
    results = []
    for level in range(ITERS):
        factor = 1.0 if level == 0 else 1.0 / stretch
        partial_value = jnp.dot(matrix, current, preferred_element_type=jnp.float32)
        portion = summed_on_arrival(partial_value, "col", 0)
        reduced = collect((portion * factor).astype(jnp.bfloat16), "col", 0)
        whole_term = lax.dot_general(
            matrix, reduced, (((0,), (0,)), ((), ())), preferred_element_type=jnp.float32
        )
        portion = summed_rows(whole_term, ROW, (1, 0), 0)
        current = collect((portion * stretch).astype(jnp.bfloat16), ROW, 0)
        results.append(current)
    return jnp.stack(results)


def solution(mesh):
    torus = Mesh(mesh.devices.reshape(2, 4, mesh.shape["col"]), ("row_0", "row_1", "col"))
    placed = (P(ROW, "col"), P("col", None))
    return jax.shard_map(
        body, mesh=torus, in_specs=placed, out_specs=P(None, "col", None), check_vma=False
    )
```

profile of v0, /device:TPU:32, one launch (start us, length us, event | category | flops | bytes accessed | tf_op | source)
XLA Modules:
  0.0 415.3 jit_solution(13337614375595336923)
XLA Ops:
  6.5 0.0 copy-start
  6.5 0.0 reduce-scatter.5.cloned.1.call-start
  6.5 1.6 copy-done
  8.1 4.6 %fusion.2 = f32[384,128]{1,0:T(8,128)S(1)} fusion(bf16[384,8192]{1,0:T(8,128)(2,1)} %param.2, bf16[8192,128]{1,0:T(8,128)(2,1)S(1)} %copy-done), kind=kOutput, calls=%fused_computation.9 | convolution fusion | flops 805306368 | bytes 8585216 | tf_op jit(solution)/shard_map/dot_general | solution.py:63
  12.7 18.6 %all_to_all.30 = f32[32,12,128]{2,1,0:T(8,128)S(1)} all-to-all(f32[32,12,128]{2,1,0:T(8,128)S(1)} %reshape.28), channel_id=1, replica_groups=mesh['row_0'=2,'row_1'=4,'col'=32] {'col'}, dimensions={0} | all-to-all | bytes 393216 | tf_op jit(solution)/shard_map/all_to_all | solution.py:20
  31.4 12.1 %all_to_all.31 = bf16[32,12,128]{2,1,0:T(8,128)(2,1)S(1)} all-to-all(bf16[32,12,128]{2,1,0:T(8,128)(2,1)S(1)} %broadcast_in_dim.12), channel_id=1, replica_groups=mesh['row_0'=2,'row_1'=4,'col'=32] {'col'}, dimensions={0} | all-to-all | bytes 196608 | tf_op jit(solution)/shard_map/all_to_all | solution.py:32
  43.5 6.1 %convolution_bitcast_fusion.1 = f32[8192,128]{0,1:T(8,128)} fusion(bf16[384,128]{1,0:T(8,128)(2,1)S(1)} %reshape.29, bf16[384,8192]{1,0:T(8,128)(2,1)} %param.2), kind=kOutput, calls=%fused_computation.1 | convolution fusion | flops 805306368 | bytes 10584064 | tf_op jit(solution)/shard_map/dot_general | solution.py:66
  49.6 6.0 %reshape_reshape.6 = f32[2,4,1024,128]{2,1,0,3:T(4,128)} reshape(f32[8192,128]{0,1:T(8,128)} %convolution_bitcast_fusion.1) | data formatting | bytes 8388608 | tf_op jit(solution)/shard_map/reshape;reshape | solution.py:43
  55.7 5.3 %copy.3 = f32[2,4,1024,128]{3,2,0,1:T(8,128)} copy(f32[2,4,1024,128]{2,1,0,3:T(4,128)} %reshape_reshape.6) | data formatting | bytes 8388608 | tf_op jit(solution)/shard_map/reshape;reshape | solution.py:43
  61.0 0.0 reduce-scatter.5.cloned.1.call-update
  61.0 0.0 reduce-scatter.7.cloned.1.call-start
  61.0 48.7 %reduce-scatter.5.cloned.1.call-done = f32[2,1024,128]{2,1,0:T(8,128)} async-done(((f32[8,1024,128]{2,1,0:T(8,128)}), f32[2,1024,128]{2,1,0:T(8,128)}) %reduce-scatter.5.cloned.1.call-update) | async-done | bytes 1048592 | tf_op jit(solution)/shard_map/reduce_scatter | solution.py:46
  109.7 0.0 reduce-scatter.7.cloned.1.call-update
  109.7 0.0 reduce-scatter.9.cloned.1.call-start
  109.8 42.1 %reduce-scatter.7.cloned.1.call-done = f32[1,1024,128]{2,1,0:T(8,128)} async-done(((f32[2,1024,128]{2,1,0:T(8,128)}), f32[1,1024,128]{2,1,0:T(8,128)}) %reduce-scatter.7.cloned.1.call-update) | async-done | bytes 524304 | tf_op jit(solution)/shard_map/reduce_scatter | solution.py:46
  151.9 1.1 fusion
  153.0 0.3 broadcast_in_dim.14
  153.3 57.0 %all_to_all.32 = bf16[8,1024,128]{2,1,0:T(8,128)(2,1)S(1)} all-to-all(bf16[8,1024,128]{2,1,0:T(8,128)(2,1)S(1)} %broadcast_in_dim.14), channel_id=1, replica_groups=mesh['row_0'=2,'row_1'=4,'col'=32] {'row_0','row_1'}, dimensions={0} | all-to-all | bytes 4194304 | tf_op jit(solution)/shard_map/all_to_all | solution.py:32
  210.2 0.0 copy-start.1
  210.2 1.3 copy-done.1
  211.5 4.9 %convolution_bitcast_fusion.2 = f32[384,128]{0,1:T(8,128)S(1)} fusion(bf16[8192,128]{1,0:T(8,128)(2,1)S(1)} %bitcast.31, bf16[384,8192]{1,0:T(8,128)(2,1)} %param.2), kind=kOutput, calls=%fused_computation.3 | convolution fusion | flops 805306368 | bytes 8585216 | tf_op jit(solution)/shard_map/dot_general | solution.py:63
  216.4 0.1 copy.4
  216.6 15.7 %all_to_all.33 = f32[32,12,128]{2,1,0:T(8,128)S(1)} all-to-all(f32[32,12,128]{2,1,0:T(8,128)S(1)} %reshape.32), channel_id=1, replica_groups=mesh['row_0'=2,'row_1'=4,'col'=32] {'col'}, dimensions={0} | all-to-all | bytes 393216 | tf_op jit(solution)/shard_map/all_to_all | solution.py:20
  232.4 12.1 %all_to_all.34 = bf16[32,12,128]{2,1,0:T(8,128)(2,1)S(1)} all-to-all(bf16[32,12,128]{2,1,0:T(8,128)(2,1)S(1)} %broadcast_in_dim.15), channel_id=1, replica_groups=mesh['row_0'=2,'row_1'=4,'col'=32] {'col'}, dimensions={0} | all-to-all | bytes 196608 | tf_op jit(solution)/shard_map/all_to_all | solution.py:32
  244.5 6.1 %convolution_bitcast_fusion = f32[8192,128]{0,1:T(8,128)} fusion(bf16[384,128]{1,0:T(8,128)(2,1)S(1)} %reshape.33, bf16[384,8192]{1,0:T(8,128)(2,1)} %param.2), kind=kOutput, calls=%fused_computation | convolution fusion | flops 805306368 | bytes 10584064 | tf_op jit(solution)/shard_map/dot_general | solution.py:66
  250.6 6.0 %reshape_reshape.7 = f32[2,4,1024,128]{2,1,0,3:T(4,128)} reshape(f32[8192,128]{0,1:T(8,128)} %convolution_bitcast_fusion) | data formatting | bytes 8388608 | tf_op jit(solution)/shard_map/reshape;reshape | solution.py:43
  256.6 5.3 %copy.5 = f32[2,4,1024,128]{3,2,0,1:T(8,128)} copy(f32[2,4,1024,128]{2,1,0,3:T(4,128)} %reshape_reshape.7) | data formatting | bytes 8388608 | tf_op jit(solution)/shard_map/reshape;reshape | solution.py:43
  261.9 0.0 reduce-scatter.9.cloned.1.call-update
  261.9 0.0 reduce-scatter.11.cloned.1.call-start
  262.0 43.9 %reduce-scatter.9.cloned.1.call-done = f32[2,1024,128]{2,1,0:T(8,128)} async-done(((f32[8,1024,128]{2,1,0:T(8,128)}), f32[2,1024,128]{2,1,0:T(8,128)}) %reduce-scatter.9.cloned.1.call-update) | async-done | bytes 1048592 | tf_op jit(solution)/shard_map/reduce_scatter | solution.py:46
  305.9 0.0 reduce-scatter.11.cloned.1.call-update
  306.0 42.0 %reduce-scatter.11.cloned.1.call-done = f32[1,1024,128]{2,1,0:T(8,128)} async-done(((f32[2,1024,128]{2,1,0:T(8,128)}), f32[1,1024,128]{2,1,0:T(8,128)}) %reduce-scatter.11.cloned.1.call-update) | async-done | bytes 524304 | tf_op jit(solution)/shard_map/reduce_scatter | solution.py:46
  348.0 0.0 copy-start.2
  348.0 1.2 fusion.1
  349.2 0.3 broadcast_in_dim.33
  349.5 57.0 %all_to_all.35 = bf16[8,1024,128]{2,1,0:T(8,128)(2,1)S(1)} all-to-all(bf16[8,1024,128]{2,1,0:T(8,128)(2,1)S(1)} %broadcast_in_dim.33), channel_id=1, replica_groups=mesh['row_0'=2,'row_1'=4,'col'=32] {'row_0','row_1'}, dimensions={0} | all-to-all | bytes 4194304 | tf_op jit(solution)/shard_map/all_to_all | solution.py:32
  406.4 0.0 copy-done.2
  406.4 2.4 pad_maximum_fusion
  (9 shorter events, 0.2 us)
Async XLA Ops:
  6.5 1.6 copy-start
  6.5 103.2 %reduce-scatter.5.cloned.1.call-start = ((), (), s32[]{:S(2)}) async-start(), calls=%async_computation.10 | async-start | bytes 5242880 | tf_op jit(solution)/shard_map/reduce_scatter | solution.py:46
  61.0 90.9 %reduce-scatter.7.cloned.1.call-start = ((), (), s32[]{:S(2)}) async-start(), calls=%async_computation.11 | async-start | bytes 1572864 | tf_op jit(solution)/shard_map/reduce_scatter | solution.py:46
  109.7 196.2 %reduce-scatter.9.cloned.1.call-start = ((), (), s32[]{:S(2)}) async-start(), calls=%async_computation.12 | async-start | bytes 5242880 | tf_op jit(solution)/shard_map/reduce_scatter | solution.py:46
  210.2 1.3 copy-start.1
  261.9 86.0 %reduce-scatter.11.cloned.1.call-start = ((), (), s32[]{:S(2)}) async-start(), calls=%async_computation.13 | async-start | bytes 1572864 | tf_op jit(solution)/shard_map/reduce_scatter | solution.py:46
  348.0 58.5 %copy-start.2 = (bf16[8,1024,128]{2,1,0:T(8,128)(2,1)S(1)}, bf16[8,1024,128]{2,1,0:T(8,128)(2,1)}, u32[]{:S(2)}) copy-start(bf16[8,1024,128]{2,1,0:T(8,128)(2,1)} %copy-done.1) | copy-start | bytes 6291460
Sparse Core Ops, SparseCore 0:
  61.1 48.5 reduce-scatter.4
  112.2 39.6 reduce-scatter.6
  262.1 43.8 reduce-scatter.8
  308.3 39.6 reduce-scatter.10
where the time goes:
time: 416 us; the launch traced here: 415 us
  waiting for transfers between devices  177 us (43%)
  blocking collectives  172 us (41%)
  local copies, waits for them, and re-layouts  26.4 us (6%)
  matrix products  21.6 us (5%)
  between operations  13.2 us (3%)
  other arithmetic  4.77 us (1%)
    reduce_scatter x4, waiting for transfers between devices, sum_in_order(): blocks = lax.psum_scatter(blocks, axes[k], scatter_dimension=0, tiled=True)  177 us
    all_to_all x4, blocking collectives, copy_for_each(): lax.all_to_all(jnp.broadcast_to(shard[None], (length, *shard.shape)), axi...  138 us
    all_to_all x2, blocking collectives, summed_on_arrival(): lax.all_to_all(blocks, axis, split_axis=0, concat_axis=0, tiled=True)  34.4 us
    another operation x4, local copies, waits for them, and re-layouts, sum_in_order(): blocks = blocks.reshape(*(lax.axis_size(a) for a in axes), *inside)  22.6 us
    dot_general x2, matrix products, body(): lax.dot_general(matrix, reduced, (((0,), (0,)), ((), ())), preferred_elem...  12.2 us
    dot_general x2, matrix products, body(): partial_value = jnp.dot(matrix, current, preferred_element_type=jnp.float32)  9.41 us
  transfers between devices with their start and end apart: 4, of which 4 were waited for; matrix products, arithmetic and copies ran while one was open for 0% of the time, Pallas kernels for 0%

commit v1 on v0

v1 whole, which is shorter than its diff:
```python
import functools
import math

import jax
import jax.numpy as jnp
from jax import lax
from jax.experimental import pallas as pl
from jax.experimental.pallas import tpu as pltpu
from jax.sharding import Mesh
from jax.sharding import PartitionSpec as P

AXES = ("zh", "x", "zl", "y", "core")
SIZES = (2, 4, 4, 4, 2)
NX, NZL, NY, NC = 4, 4, 4, 2
ITERS = 2
STREAMS = 4
LOADS = 8
F32, BF16 = jnp.float32, jnp.bfloat16
MESH_ID = pl.DeviceIdType.MESH


def kernel(
    stretch,
    a_hbm, p_hbm, out,
    a, p, z1, zsend, zr1, zs2, zr2, zg, ysend, yown, yr, hs, hr,
    load_sem, send_sem, recv_sem,
):
    rows, width = a.shape
    group = width // NX
    depth = out.shape[2] // STREAMS
    part = depth // NY
    step = width // LOADS
    x, zl, y, core = (lax.axis_index(n) for n in ("x", "zl", "y", "core"))
    zh = lax.axis_index("zh")
    me = y * NC + core

    def columns(b):
        return pl.ds(b * step, step)

    loads = []
    for b in range(LOADS):
        pair = (
            pltpu.make_async_copy(a_hbm.at[:, columns(b)], a.at[:, columns(b)], load_sem.at[0, b]),
            pltpu.make_async_copy(p_hbm.at[columns(b)], p.at[columns(b)], load_sem.at[1, b]),
        )
        for copy in pair:
            copy.start()
        loads.append(pair)

    near = [(dy, dc) for dy in range(NY) for dc in range(NC) if dy or dc]

    def near_id(dy, dc):
        return {"y": lax.rem(y + dy, NY), "core": lax.rem(core + dc, NC)}

    def x_id(dx):
        return {"x": lax.rem(x + dx, NX)}

    def zl_id(dz):
        return {"zl": lax.rem(zl + dz, NZL)}

    def y_id(dy):
        return {"y": lax.rem(y + dy, NY)}

    half_id = {"zh": 1 - zh}
    x_order = (2, 1, 3)

    barrier = pltpu.get_barrier_semaphore()
    peers = [near_id(*d) for d in near] + [zl_id(d) for d in (1, 2, 3)]
    peers += [x_id(d) for d in (1, 2, 3)] + [half_id]
    for peer in peers:
        pl.semaphore_signal(barrier, inc=1, device_id=peer, device_id_type=MESH_ID)

    def send(src, dst, j, stage, peer):
        pltpu.make_async_remote_copy(
            src_ref=src, dst_ref=dst, send_sem=send_sem.at[j, stage], recv_sem=recv_sem.at[j, stage],
            device_id=peer, device_id_type=MESH_ID,
        ).start()

    def done(ref, j, stage):
        return pltpu.make_async_remote_copy(
            src_ref=ref, dst_ref=ref, send_sem=send_sem.at[j, stage], recv_sem=recv_sem.at[j, stage],
            device_id=half_id, device_id_type=MESH_ID,
        )

    def stream_rows(s):
        return pl.ds(s * depth, depth)

    def z_send(j, value):
        zsend[j] = value.reshape(NY, part, rows)
        zr1[j, me] = zsend[j, y]
        for dy, dc in near:
            peer = near_id(dy, dc)
            send(zsend.at[j, peer["y"]], zr1.at[j, me], j, 0, peer)

    def t1(s):
        j = STREAMS + s
        done(out.at[0, pl.ds(0, NX - 1), stream_rows(s)], s, 5).wait_recv()
        total = jnp.zeros((depth, rows), F32)
        for b in range(NX):
            total += lax.dot_general(
                out[0, b, stream_rows(s), :], a[:, pl.ds(b * group, group)],
                (((1,), (1,)), ((), ())), preferred_element_type=F32,
            )
        z_send(j, total)

    def t2(j):
        done(zr1.at[j, pl.ds(0, NY * NC - 1)], j, 0).wait_recv()
        total = zr1[j, 0]
        for i in range(1, NY * NC):
            total += zr1[j, i]
        zs2[j] = total
        zr2[j, zl] = total
        for dz in (1, 2, 3):
            send(zs2.at[j], zr2.at[j, zl], j, 1, zl_id(dz))

    def t3(j, factor):
        done(zr2.at[j, pl.ds(0, NZL - 1)], j, 1).wait_recv()
        total = zr2[j, 0]
        for i in range(1, NZL):
            total += zr2[j, i]
        zg[j, y] = (total * factor).astype(BF16).astype(F32)
        for dy in (1, 2, 3):
            send(zg.at[j, y], zg.at[j, y], j, 2, y_id(dy))

    def t4(j):
        done(zg.at[j, pl.ds(0, NY - 1)], j, 2).wait_recv()
        z = zg[j].reshape(depth, rows).astype(BF16)

        def block(owner):
            return jnp.dot(
                z, a[:, pl.ds(pl.multiple_of(owner * group, group), group)],
                preferred_element_type=F32,
            )

        for i, dx in enumerate(x_order):
            ysend[j, i] = block(lax.rem(x + dx, NX)).astype(BF16)
            send(ysend.at[j, i], yr.at[j, i], j, 3, x_id(dx))
        yown[j] = block(x)

    def t5(j):
        done(yr.at[j], j, 3).wait_recv()
        total = yown[j]
        for i in range(NX - 1):
            total += yr[j, i].astype(F32)
        hs[j] = total.astype(BF16)
        send(hs.at[j], hr.at[j], j, 4, half_id)

    def t6(k, s):
        j = k * STREAMS + s
        done(hr.at[j], j, 4).wait_recv()
        total = (hs[j].astype(F32) + hr[j].astype(F32)) * stretch
        place = out.at[k, x, stream_rows(s)]
        out[k, x, stream_rows(s), :] = total.astype(BF16)
        for dx in x_order:
            send(place, place, j, 5, x_id(dx))

    for b in range(LOADS):
        for copy in loads[b]:
            copy.wait()
        term = jnp.dot(a[:, columns(b)], p[columns(b), :], preferred_element_type=F32)
        if b == 0:
            z1[...] = term
        else:
            z1[...] += term
    first = z1[...].T
    pl.semaphore_wait(barrier, len(peers))

    S = STREAMS
    for s in range(S):
        z_send(s, first[s * depth : (s + 1) * depth])
    for s in range(S):
        t2(s)
    for s in range(S):
        t3(s, 1.0)
    for s in range(S):
        t4(s)
    inv = 1.0 / stretch
    plan = (
        50, 51, 60, 52, 61, 53, 62, 10, 63, 11, 24, 12, 34, 25, 44, 13, 35, 26,
        45, 27, 36, 54, 46, 37, 55, 47, 64, 56, 65, 57, 66, 67,
    )
    for task in plan:
        kind, j = divmod(task, 10)
        if kind == 1:
            t1(j)
        elif kind == 2:
            t2(j)
        elif kind == 3:
            t3(j, inv)
        elif kind == 4:
            t4(j)
        elif kind == 5:
            t5(j)
        else:
            t6(*divmod(j, S))
    for s in range(S):
        done(out.at[1, pl.ds(0, NX - 1), stream_rows(s)], S + s, 5).wait_recv()
    for j in range(ITERS * S):
        for stage, ref in enumerate(
            (
                zr1.at[j, pl.ds(0, NY * NC - 1)], zr2.at[j, pl.ds(0, NZL - 1)], zg.at[j, pl.ds(0, NY - 1)],
                ysend.at[j], hs.at[j], out.at[0, pl.ds(0, NX - 1), stream_rows(0)],
            )
        ):
            done(ref, j, stage).wait_send()


def body(matrix, probes):
    rows, width = matrix.shape
    probe = probes.shape[1]
    m_total = rows * SIZES[0] * SIZES[1]
    n_total = width * SIZES[2] * SIZES[3] * SIZES[4]
    group, depth = width // NX, probe // STREAMS
    part, count = depth // NY, ITERS * STREAMS
    blocks = pl.pallas_call(
        functools.partial(kernel, math.sqrt(n_total / m_total)),
        out_shape=jax.ShapeDtypeStruct((ITERS, NX, probe, group), BF16),
        in_specs=[pl.BlockSpec(memory_space=pl.ANY)] * 2,
        out_specs=pl.BlockSpec(memory_space=pltpu.VMEM),
        scratch_shapes=[
            pltpu.VMEM((rows, width), BF16),
            pltpu.VMEM((width, probe), BF16),
            pltpu.VMEM((rows, probe), F32),
            pltpu.VMEM((count, NY, part, rows), F32),
            pltpu.VMEM((count, NY * NC, part, rows), F32),
            pltpu.VMEM((count, part, rows), F32),
            pltpu.VMEM((count, NZL, part, rows), F32),
            pltpu.VMEM((count, NY, part, rows), F32),
            pltpu.VMEM((count, NX - 1, depth, group), BF16),
            pltpu.VMEM((count, depth, group), F32),
            pltpu.VMEM((count, NX - 1, depth, group), BF16),
            pltpu.VMEM((count, depth, group), BF16),
            pltpu.VMEM((count, depth, group), BF16),
            pltpu.SemaphoreType.DMA((2, LOADS)),
            pltpu.SemaphoreType.DMA((count, 6)),
            pltpu.SemaphoreType.DMA((count, 6)),
        ],
        compiler_params=pltpu.CompilerParams(
            collective_id=0, has_side_effects=True, vmem_limit_bytes=56 * 1024 * 1024
        ),
    )(matrix, probes)
    return jnp.swapaxes(blocks, 2, 3).reshape(ITERS, width, probe)


def solution(mesh):
    torus = Mesh(mesh.devices.reshape(SIZES), AXES)
    col = ("zl", "y", "core")
    return jax.shard_map(
        body, mesh=torus, in_specs=(P(("zh", "x"), col), P(col, None)),
        out_specs=P(None, col, None), check_vma=False,
    )
```

time: 416 us -> 131 us (0.31)
  waiting for transfers between devices: 177 us -> 0 us
  blocking collectives: 172 us -> 0 us
  Pallas kernels: 0 us -> 124 us
  matrix products: 21.6 us -> 0 us
  local copies, waits for them, and re-layouts: 26.4 us -> 6.2 us
  between operations: 13.2 us -> 0.01 us
  other arithmetic: 4.77 us -> 0 us
    reduce_scatter x4 -> x0, waiting for transfers between devices: 177 us -> none  [sum_in_order(): blocks = lax.psum_scatter(blocks, axes[k], scatter_dimension=0, tiled=True)]
    all_to_all x6 -> x0, blocking collectives: 172 us -> none  [the longest x4 138 us: copy_for_each(): lax.all_to_all(jnp.broadcast_to(shard[None], (length, *shard.shape)), axi...]
    pallas_call x0 -> x1, Pallas kernels: none -> 124 us  [body(): pl.pallas_call(functools.partial(kernel, math.sqrt(n_total / m_total)), o...]
    another operation x4 -> x0, local copies, waits for them, and re-layouts: 22.6 us -> none  [sum_in_order(): blocks = blocks.reshape(*(lax.axis_size(a) for a in axes), *inside)]
    dot_general x4 -> x0, matrix products: 21.6 us -> none  [the longest x2 12.2 us: body(): lax.dot_general(matrix, reduced, (((0,), (0,)), ((), ())), preferred_elem...]
    transpose x0 -> x1, local copies, waits for them, and re-layouts: none -> 6.2 us  [body(): return jnp.swapaxes(blocks, 2, 3).reshape(ITERS, width, probe)]
  transfers between devices with their start and end apart: 4 -> 0, of which waited for: 4 -> 0; matrix products, arithmetic and copies ran while one was open for 0% -> 0% of each run, Pallas kernels for 0% -> 0%
where the time goes in v1:
time: 131 us; the launch traced here: 130 us
  Pallas kernels  124 us (95%)
  local copies, waits for them, and re-layouts  6.2 us (5%)
    pallas_call x1, Pallas kernels, body(): pl.pallas_call(functools.partial(kernel, math.sqrt(n_total / m_total)), o...  124 us
    transpose x1, local copies, waits for them, and re-layouts, body(): return jnp.swapaxes(blocks, 2, 3).reshape(ITERS, width, probe)  6.2 us

profile of v1, /device:TPU:32, one launch (start us, length us, event | category | flops | bytes accessed | tf_op | source)
XLA Modules:
  0.0 130.5 jit_solution(8780762522044741021)
XLA Ops:
  0.0 124.3 %shard_map.28 = bf16[2,4,128,2048]{3,2,1,0:T(8,128)(2,1)} custom-call(bf16[384,8192]{1,0:T(8,128)(2,1)} %a_hbm.1, bf16[8192,128]{1,0:T(8,128)(2,1)} %p_hbm.1), custom_call_target="tpu_custom_call" | custom-call | tf_op jit(solution)/shard_map/pallas_call | solution.py:215
  124.3 6.2 %copy.3 = bf16[2,4,2048,128]{3,2,1,0:T(8,128)(2,1)} copy(bf16[2,4,2048,128]{2,3,1,0:T(8,128)(2,1)} %bitcast.2) | data formatting | bytes 8388608 | tf_op jit(solution)/shard_map/transpose | solution.py:242

commit v2 on v1

v2 whole, which is shorter than its diff:
```python
import functools
import math

import jax
import jax.numpy as jnp
from jax import lax
from jax.experimental import pallas as pl
from jax.experimental.pallas import tpu as pltpu
from jax.sharding import Mesh
from jax.sharding import PartitionSpec as P

AXES = ("zh", "x", "zl", "y", "core")
SIZES = (2, 4, 4, 4, 2)
NX, NZL, NY, NC = 4, 4, 4, 2
ITERS = 2
STREAMS = 4
PARTS = 2
LOADS = 8
PLAN = (
    0, 1, 2, 3, 1000, 1001, 1002, 1003, 200, 201, 202, 203, 300, 301, 302, 303, 400, 900, 401, 402, 901, 403, 500,
    902, 501, 903, 502, 503, 504, 505, 506, 507, 600, 601, 602, 603, 604, 700, 605, 606, 607, 701, 800, 702, 801,
    703, 802, 104, 704, 803, 705, 804, 105, 204, 706, 805, 707, 806, 106, 304, 205, 807, 107, 305, 404, 206, 904,
    508, 405, 509, 306, 905, 207, 608, 510, 406, 906, 511, 609, 307, 610, 512, 513, 708, 407, 907, 611, 709, 612,
    613, 808, 710, 514, 515, 711, 809, 712, 810, 614, 615, 713, 811, 812, 813, 714, 715, 814, 815,
)
F32, BF16 = jnp.float32, jnp.bfloat16
MESH_ID = pl.DeviceIdType.MESH


def kernel(
    stretch,
    a_hbm, p_hbm, out,
    a, at, p, z1, zpart, zsend, zr1, zs2, zr2, zg, far, alone, held, yown, passed, yr, hs, hr,
    load_sem, z_send_sem, z_recv_sem, y_send_sem, y_recv_sem,
):
    rows, width = a.shape
    group = width // NX
    half = group // 2
    depth = out.shape[2] // STREAMS
    part = depth // NY
    sub = depth // PARTS
    step = width // LOADS
    x, zl, y, core = (lax.axis_index(n) for n in ("x", "zl", "y", "core"))
    zh = lax.axis_index("zh")
    me = y * NC + core

    def columns(b):
        return pl.ds(b * step, step)

    loads = []
    for b in range(LOADS):
        pair = (
            pltpu.make_async_copy(a_hbm.at[:, columns(b)], a.at[:, columns(b)], load_sem.at[0, b]),
            pltpu.make_async_copy(p_hbm.at[columns(b)], p.at[columns(b)], load_sem.at[1, b]),
        )
        for copy in pair:
            copy.start()
        loads.append(pair)

    near = [(dy, dc) for dy in range(NY) for dc in range(NC) if dy or dc]

    def near_id(dy, dc):
        return {"y": lax.rem(y + dy, NY), "core": lax.rem(core + dc, NC)}

    def x_id(dx):
        return {"x": lax.rem(x + dx, NX)}

    def zl_id(dz):
        return {"zl": lax.rem(zl + dz, NZL)}

    def y_id(dy):
        return {"y": lax.rem(y + dy, NY)}

    other = {"zh": 1 - zh}
    right, left = x_id(1), x_id(3)

    barrier = pltpu.get_barrier_semaphore()
    peers = [near_id(*d) for d in near] + [zl_id(d) for d in (1, 2, 3)]
    peers += [x_id(d) for d in (1, 2, 3)] + [other]
    for peer in peers:
        pl.semaphore_signal(barrier, inc=1, device_id=peer, device_id_type=MESH_ID)

    sent, got = {}, set()
    low, high = pl.ds(0, half), pl.ds(half, half)

    def sems(j, stage):
        if stage < 3:
            return {"send_sem": z_send_sem.at[j, stage], "recv_sem": z_recv_sem.at[j, stage]}
        return {"send_sem": y_send_sem.at[j, stage - 3], "recv_sem": y_recv_sem.at[j, stage - 3]}

    def send(src, dst, j, stage, peer):
        sent[j, stage] = 1
        pltpu.make_async_remote_copy(
            src_ref=src, dst_ref=dst, device_id=peer, device_id_type=MESH_ID, **sems(j, stage)
        ).start()

    def done(j, stage):
        r = pl.ds(0, sub)
        ref = (
            lambda: zr1.at[j, pl.ds(0, NY * NC - 1)], lambda: zr2.at[j, pl.ds(0, NZL - 1)],
            lambda: zg.at[j, pl.ds(0, NY - 1)], lambda: passed.at[j], lambda: yr.at[j], lambda: hr.at[j],
            lambda: out.at[0, pl.ds(0, 2), r], lambda: out.at[0, 0, r],
        )[stage]()
        return pltpu.make_async_remote_copy(
            src_ref=ref, dst_ref=ref, device_id=other, device_id_type=MESH_ID, **sems(j, stage)
        )

    def arrived(j, stage):
        got.add((j, stage))
        done(j, stage).wait_recv()

    def stream_rows(s):
        return pl.ds(s * depth, depth)

    def place_of(i):
        j, h = divmod(i, PARTS)
        k, s = divmod(j, STREAMS)
        return k, s, h == PARTS - 1, pl.ds(s * depth + h * sub, sub)

    def z_send(j, value):
        zsend[j] = value.reshape(NY, part, rows)
        zr1[j, me] = zsend[j, y]
        for dy, dc in near:
            peer = near_id(dy, dc)
            send(zsend.at[j, peer["y"]], zr1.at[j, me], j, 0, peer)

    def term(s, owner):
        return jnp.dot(
            out[0, owner, stream_rows(s), :], at[pl.ds(pl.multiple_of(owner * group, group), group), :],
            preferred_element_type=F32,
        )

    def t1(j):
        s = j - STREAMS

        for h in range(PARTS):
            arrived(s * PARTS + h, 7)
        z_send(j, zpart[s] + term(s, lax.rem(x + 2, NX)))

    def t2(j):
        arrived(j, 0)
        total = zr1[j, 0]
        for i in range(1, NY * NC):
            total += zr1[j, i]
        zs2[j] = total
        zr2[j, zl] = total
        for dz in (1, 2, 3):
            send(zs2.at[j], zr2.at[j, zl], j, 1, zl_id(dz))

    def t3(j):
        arrived(j, 1)
        total = zr2[j, 0]
        for i in range(1, NZL):
            total += zr2[j, i]
        factor = 1.0 if j < STREAMS else 1.0 / stretch
        zg[j, y] = (total * factor).astype(BF16).astype(F32)
        for dy in (1, 2, 3):
            send(zg.at[j, y], zg.at[j, y], j, 2, y_id(dy))

    def block(j, owner):
        z = zg[j].reshape(depth, rows).astype(BF16)
        return jnp.dot(
            z, a[:, pl.ds(pl.multiple_of(owner * group, group), group)],
            preferred_element_type=F32,
        )

    def pieces(j):
        return [(j * PARTS + h, slice(h * sub, (h + 1) * sub)) for h in range(PARTS)]

    def t4(j):
        arrived(j, 2)
        value = block(j, lax.rem(x + 2, NX)).astype(BF16)
        for i, r in pieces(j):
            far[i, 0] = value[r, :half]
            far[i, 1] = value[r, half:]
            send(far.at[i, 0], passed.at[i, 0], i, 3, right)
            send(far.at[i, 1], passed.at[i, 1], i, 3, left)

    def t9(j):
        value = block(j, right["x"])
        for i, r in pieces(j):
            held[i, 0] = value[r, :half]
            alone[i, 0] = value[r, half:].astype(BF16)
            send(alone.at[i, 0], yr.at[i, 0, 1], i, 4, right)
        value = block(j, left["x"])
        for i, r in pieces(j):
            held[i, 1] = value[r, half:]
            alone[i, 1] = value[r, :half].astype(BF16)
            send(alone.at[i, 1], yr.at[i, 1, 0], i, 4, left)
        value = block(j, x)
        for i, r in pieces(j):
            yown[i] = value[r]

    def t5(i):
        arrived(i, 3)
        for n, peer in enumerate((right, left)):
            far[i, 2 + n] = (held[i, n] + passed[i, n].astype(F32)).astype(BF16)
            send(far.at[i, 2 + n], yr.at[i, n, n], i, 4, peer)

    def t6(i):
        arrived(i, 4)
        for n, cols in enumerate((low, high)):
            total = yown[i, :, cols] + yr[i, 0, n].astype(F32) + yr[i, 1, n].astype(F32)
            hs[i, :, cols] = total.astype(BF16)
        send(hs.at[i], hr.at[i], i, 5, other)

    def t7(i):
        k, s, last, r = place_of(i)
        arrived(i, 5)
        total = (hs[i].astype(F32) + hr[i].astype(F32)) * stretch
        out[k, x, r, :] = total.astype(BF16)
        place = out.at[k, x, r]
        for peer in (right, left):
            send(place, place, i, 6, peer)
        if k == 0 and last:
            zpart[s] = term(s, x)

    def t8(i):
        k, s, last, r = place_of(i)
        arrived(i, 6)
        for source, cols, peer in ((left, low, right), (right, high, left)):
            place = out.at[k, source["x"], r, cols]
            send(place, place, i, 7, peer)
        if k == 0 and last:
            zpart[s] += term(s, right["x"]) + term(s, left["x"])

    for b in range(LOADS):
        for copy in loads[b]:
            copy.wait()
        product = jnp.dot(a[:, columns(b)], p[columns(b), :], preferred_element_type=F32)
        if b == 0:
            z1[...] = product
        else:
            z1[...] += product
    first = z1[...].T
    pl.semaphore_wait(barrier, len(peers))

    def t0(j):
        z_send(j, first[j * depth : (j + 1) * depth])

    def t10(q):
        cols = pl.ds(q * group, group)
        at[cols, :] = a[:, cols].T

    tasks = (t0, t1, t2, t3, t4, t5, t6, t7, t8, t9, t10)
    for task in PLAN:
        kind, j = divmod(task, 100)
        tasks[kind](j)
    for j, stage in sent:
        if (j, stage) not in got:
            arrived(j, stage)
    for j, stage in sent:
        done(j, stage).wait_send()


def turn(blocks, out, turned, sems):
    group = blocks.shape[3]
    copies = []
    for k in range(ITERS):
        for b in range(NX):
            rows = pl.ds(b * group, group)
            turned[k, rows, :] = blocks[k, b].T
            copy = pltpu.make_async_copy(turned.at[k, rows], out.at[k, rows], sems.at[k, b])
            copy.start()
            copies.append(copy)
    for copy in copies:
        copy.wait()


def body(matrix, probes):
    rows, width = matrix.shape
    probe = probes.shape[1]
    m_total = rows * SIZES[0] * SIZES[1]
    n_total = width * SIZES[2] * SIZES[3] * SIZES[4]
    group, depth = width // NX, probe // STREAMS
    part, half, count = depth // NY, group // 2, ITERS * STREAMS
    sub, pieces = depth // PARTS, ITERS * STREAMS * PARTS
    blocks = pl.pallas_call(
        functools.partial(kernel, math.sqrt(n_total / m_total)),
        out_shape=jax.ShapeDtypeStruct((ITERS, NX, probe, group), BF16),
        in_specs=[pl.BlockSpec(memory_space=pltpu.HBM)] * 2,
        out_specs=pl.BlockSpec(memory_space=pltpu.VMEM),
        scratch_shapes=[
            pltpu.VMEM((rows, width), BF16),
            pltpu.VMEM((width, rows), BF16),
            pltpu.VMEM((width, probe), BF16),
            pltpu.VMEM((rows, probe), F32),
            pltpu.VMEM((STREAMS, depth, rows), F32),
            pltpu.VMEM((count, NY, part, rows), F32),
            pltpu.VMEM((count, NY * NC, part, rows), F32),
            pltpu.VMEM((count, part, rows), F32),
            pltpu.VMEM((count, NZL, part, rows), F32),
            pltpu.VMEM((count, NY, part, rows), F32),
            pltpu.VMEM((pieces, 4, sub, half), BF16),
            pltpu.VMEM((pieces, 2, sub, half), BF16),
            pltpu.VMEM((pieces, 2, sub, half), F32),
            pltpu.VMEM((pieces, sub, group), F32),
            pltpu.VMEM((pieces, 2, sub, half), BF16),
            pltpu.VMEM((pieces, 2, 2, sub, half), BF16),
            pltpu.VMEM((pieces, sub, group), BF16),
            pltpu.VMEM((pieces, sub, group), BF16),
            pltpu.SemaphoreType.DMA((2, LOADS)),
            pltpu.SemaphoreType.DMA((count, 3)),
            pltpu.SemaphoreType.DMA((count, 3)),
            pltpu.SemaphoreType.DMA((pieces, 5)),
            pltpu.SemaphoreType.DMA((pieces, 5)),
        ],
        compiler_params=pltpu.CompilerParams(
            collective_id=0, has_side_effects=True, vmem_limit_bytes=44 * 1024 * 1024
        ),
    )(*(pltpu.with_memory_space_constraint(v, pltpu.HBM) for v in (matrix, probes)))
    return pl.pallas_call(
        turn,
        out_shape=jax.ShapeDtypeStruct((ITERS, width, probe), BF16),
        in_specs=[pl.BlockSpec(memory_space=pltpu.VMEM)],
        out_specs=pl.BlockSpec(memory_space=pl.ANY),
        scratch_shapes=[
            pltpu.VMEM((ITERS, width, probe), BF16),
            pltpu.SemaphoreType.DMA((ITERS, NX)),
        ],
        compiler_params=pltpu.CompilerParams(vmem_limit_bytes=24 * 1024 * 1024),
    )(blocks)


def solution(mesh):
    torus = Mesh(mesh.devices.reshape(SIZES), AXES)
    col = ("zl", "y", "core")
    return jax.shard_map(
        body, mesh=torus, in_specs=(P(("zh", "x"), col), P(col, None)),
        out_specs=P(None, col, None), check_vma=False,
    )
```

time: 131 us -> 119 us (0.908)
  local copies, waits for them, and re-layouts: 6.2 us -> 0 us
  Pallas kernels: 124 us -> 118 us
    pallas_call x1, Pallas kernels: 124 us -> 115 us  [body(): pl.pallas_call(functools.partial(kernel, math.sqrt(n_total / m_total)), o...]
    transpose x1 -> x0, local copies, waits for them, and re-layouts: 6.2 us -> none  [body(): return jnp.swapaxes(blocks, 2, 3).reshape(ITERS, width, probe)]
    pallas_call x0 -> x1, Pallas kernels: none -> 2.26 us  [body(): pl.pallas_call(turn, out_shape=jax.ShapeDtypeStruct((ITERS, width, probe)...]
where the time goes in v2:
time: 119 us; the launch traced here: 118 us
  Pallas kernels  118 us (99%)
    pallas_call x1, Pallas kernels, body(): pl.pallas_call(functools.partial(kernel, math.sqrt(n_total / m_total)), o...  115 us

profile of v2, /device:TPU:32, one launch (start us, length us, event | category | flops | bytes accessed | tf_op | source)
XLA Modules:
  0.0 117.8 jit_solution(286314024899780602)
XLA Ops:
  0.0 115.4 %shard_map.28.blocks = bf16[2,4,128,2048]{3,2,1,0:T(8,128)(2,1)S(1)} custom-call(bf16[384,8192]{1,0:T(8,128)(2,1)} %a_hbm.1, bf16[8192,128]{1,0:T(8,128)(2,1)} %p_hbm.1), custom_call_target="tpu_custom_call" | custom-call | tf_op jit(solution)/shard_map/pallas_call | solution.py:278
  115.4 2.3 %shard_map.29 = bf16[2,8192,128]{2,1,0:T(8,128)(2,1)} custom-call(bf16[2,4,128,2048]{3,2,1,0:T(8,128)(2,1)S(1)} %shard_map.28.blocks), custom_call_target="tpu_custom_call" | custom-call | tf_op jit(solution)/shard_map/pallas_call | solution.py:312

commit v3 on v2

--- a/solution.py
+++ b/solution.py
@@ -15,13 +15,15 @@
 ITERS = 2
 STREAMS = 4
 PARTS = 2
+STRAIGHT_SUMS = (0, 1)
+STRAIGHT_COPIES = (14, 15)
 LOADS = 8
 PLAN = (
-    0, 1, 2, 3, 1000, 1001, 1002, 1003, 200, 201, 202, 203, 300, 301, 302, 303, 400, 900, 401, 402, 901, 403, 500,
-    902, 501, 903, 502, 503, 504, 505, 506, 507, 600, 601, 602, 603, 604, 700, 605, 606, 607, 701, 800, 702, 801,
-    703, 802, 104, 704, 803, 705, 804, 105, 204, 706, 805, 707, 806, 106, 304, 205, 807, 107, 305, 404, 206, 904,
-    508, 405, 509, 306, 905, 207, 608, 510, 406, 906, 511, 609, 307, 610, 512, 513, 708, 407, 907, 611, 709, 612,
-    613, 808, 710, 514, 515, 711, 809, 712, 810, 614, 615, 713, 811, 812, 813, 714, 715, 814, 815,
+    0, 1000, 1, 2, 3, 200, 201, 1003, 300, 203, 202, 400, 301, 1002, 303, 302, 900, 401, 403, 901, 600, 502, 903,
+    503, 601, 1001, 402, 602, 506, 507, 700, 603, 902, 606, 504, 701, 607, 505, 800, 702, 703, 604, 801, 605, 706,
+    803, 802, 104, 707, 704, 705, 105, 204, 806, 807, 804, 805, 205, 304, 107, 106, 305, 404, 207, 904, 206, 508,
+    405, 307, 509, 905, 510, 306, 608, 511, 407, 609, 907, 406, 611, 514, 906, 708, 610, 512, 709, 513, 614, 515,
+    808, 711, 612, 710, 809, 613, 615, 714, 712, 810, 811, 713, 812, 715, 813,
 )
 F32, BF16 = jnp.float32, jnp.bfloat16
 MESH_ID = pl.DeviceIdType.MESH
@@ -72,7 +74,7 @@
         return {"y": lax.rem(y + dy, NY)}
 
     other = {"zh": 1 - zh}
-    right, left = x_id(1), x_id(3)
+    right, left, across = x_id(1), x_id(3), x_id(2)
 
     barrier = pltpu.get_barrier_semaphore()
     peers = [near_id(*d) for d in near] + [zl_id(d) for d in (1, 2, 3)]
@@ -115,7 +117,13 @@
     def place_of(i):
         j, h = divmod(i, PARTS)
         k, s = divmod(j, STREAMS)
-        return k, s, h == PARTS - 1, pl.ds(s * depth + h * sub, sub)
+        return k, s, pl.ds(s * depth + h * sub, sub)
+
+    counts = {}
+
+    def whole(kind, s):
+        counts[kind, s] = counts.get((kind, s), 0) + 1
+        return counts[kind, s] == PARTS
 
     def z_send(j, value):
         zsend[j] = value.reshape(NY, part, rows)
@@ -135,7 +143,7 @@
 
         for h in range(PARTS):
             arrived(s * PARTS + h, 7)
-        z_send(j, zpart[s] + term(s, lax.rem(x + 2, NX)))
+        z_send(j, zpart[s] + term(s, across["x"]))
 
     def t2(j):
         arrived(j, 0)
@@ -169,22 +177,31 @@
 
     def t4(j):
         arrived(j, 2)
-        value = block(j, lax.rem(x + 2, NX)).astype(BF16)
+        value = block(j, across["x"]).astype(BF16)
         for i, r in pieces(j):
             far[i, 0] = value[r, :half]
             far[i, 1] = value[r, half:]
-            send(far.at[i, 0], passed.at[i, 0], i, 3, right)
-            send(far.at[i, 1], passed.at[i, 1], i, 3, left)
+            straight = i in STRAIGHT_SUMS
+            send(far.at[i, 0], passed.at[i, 0], i, 3, across if straight else right)
+            send(far.at[i, 1], passed.at[i, 1], i, 3, across if straight else left)
 
     def t9(j):
         value = block(j, right["x"])
         for i, r in pieces(j):
-            held[i, 0] = value[r, :half]
+            if i in STRAIGHT_SUMS:
+                far[i, 2] = value[r, :half].astype(BF16)
+                send(far.at[i, 2], yr.at[i, 0, 0], i, 4, right)
+            else:
+                held[i, 0] = value[r, :half]
             alone[i, 0] = value[r, half:].astype(BF16)
             send(alone.at[i, 0], yr.at[i, 0, 1], i, 4, right)
         value = block(j, left["x"])
         for i, r in pieces(j):
-            held[i, 1] = value[r, half:]
+            if i in STRAIGHT_SUMS:
+                far[i, 3] = value[r, half:].astype(BF16)
+                send(far.at[i, 3], yr.at[i, 1, 1], i, 4, left)
+            else:
+                held[i, 1] = value[r, half:]
             alone[i, 1] = value[r, :half].astype(BF16)
             send(alone.at[i, 1], yr.at[i, 1, 0], i, 4, left)
         value = block(j, x)
@@ -199,29 +216,37 @@
 
     def t6(i):
         arrived(i, 4)
+        if i in STRAIGHT_SUMS:
+            arrived(i, 3)
         for n, cols in enumerate((low, high)):
             total = yown[i, :, cols] + yr[i, 0, n].astype(F32) + yr[i, 1, n].astype(F32)
+            if i in STRAIGHT_SUMS:
+                total += passed[i, n].astype(F32)
             hs[i, :, cols] = total.astype(BF16)
         send(hs.at[i], hr.at[i], i, 5, other)
 
     def t7(i):
-        k, s, last, r = place_of(i)
+        k, s, r = place_of(i)
         arrived(i, 5)
         total = (hs[i].astype(F32) + hr[i].astype(F32)) * stretch
         out[k, x, r, :] = total.astype(BF16)
         place = out.at[k, x, r]
         for peer in (right, left):
             send(place, place, i, 6, peer)
-        if k == 0 and last:
+        if i in STRAIGHT_COPIES:
+            send(place, place, i, 7, across)
+        if k == 0 and whole(7, s):
             zpart[s] = term(s, x)
 
     def t8(i):
-        k, s, last, r = place_of(i)
+        k, s, r = place_of(i)
         arrived(i, 6)
         for source, cols, peer in ((left, low, right), (right, high, left)):
+            if i in STRAIGHT_COPIES:
+                break
             place = out.at[k, source["x"], r, cols]
             send(place, place, i, 7, peer)
-        if k == 0 and last:
+        if k == 0 and whole(8, s):
             zpart[s] += term(s, right["x"]) + term(s, left["x"])
 
     for b in range(LOADS):

time: 119 us -> 110 us (0.924)
  Pallas kernels: 118 us -> 110 us
    pallas_call x1, Pallas kernels: 115 us -> 107 us  [body(): pl.pallas_call(functools.partial(kernel, math.sqrt(n_total / m_total)), o...]
where the time goes in v3:
time: 110 us
  Pallas kernels  110 us (100%)
    pallas_call x1, Pallas kernels, body(): pl.pallas_call(functools.partial(kernel, math.sqrt(n_total / m_total)), o...  107 us
    pallas_call x1, Pallas kernels, body(): pl.pallas_call(turn, out_shape=jax.ShapeDtypeStruct((ITERS, width, probe)...  2.26 us

profile of v3, /device:TPU:32, one launch (start us, length us, event | category | flops | bytes accessed | tf_op | source)
XLA Modules:
  0.0 109.9 jit_solution(14217266159966715610)
XLA Ops:
  0.0 107.4 %shard_map.28.blocks = bf16[2,4,128,2048]{3,2,1,0:T(8,128)(2,1)S(1)} custom-call(bf16[384,8192]{1,0:T(8,128)(2,1)} %a_hbm.1, bf16[8192,128]{1,0:T(8,128)(2,1)} %p_hbm.1), custom_call_target="tpu_custom_call" | custom-call | tf_op jit(solution)/shard_map/pallas_call | solution.py:303
  107.4 2.3 %shard_map.29 = bf16[2,8192,128]{2,1,0:T(8,128)(2,1)} custom-call(bf16[2,4,128,2048]{3,2,1,0:T(8,128)(2,1)S(1)} %shard_map.28.blocks), custom_call_target="tpu_custom_call" | custom-call | tf_op jit(solution)/shard_map/pallas_call | solution.py:337

commit v4 on v3

--- a/solution.py
+++ b/solution.py
@@ -19,11 +19,11 @@
 STRAIGHT_COPIES = (14, 15)
 LOADS = 8
 PLAN = (
-    0, 1000, 1, 2, 3, 200, 201, 1003, 300, 203, 202, 400, 301, 1002, 303, 302, 900, 401, 403, 901, 600, 502, 903,
-    503, 601, 1001, 402, 602, 506, 507, 700, 603, 902, 606, 504, 701, 607, 505, 800, 702, 703, 604, 801, 605, 706,
-    803, 802, 104, 707, 704, 705, 105, 204, 806, 807, 804, 805, 205, 304, 107, 106, 305, 404, 207, 904, 206, 508,
-    405, 307, 509, 905, 510, 306, 608, 511, 407, 609, 907, 406, 611, 514, 906, 708, 610, 512, 709, 513, 614, 515,
-    808, 711, 612, 710, 809, 613, 615, 714, 712, 810, 811, 713, 812, 715, 813,
+    1, 0, 3, 2, 201, 200, 202, 301, 203, 300, 401, 303, 302, 400, 900, 402, 1000, 901, 1003, 502, 600, 403, 503,
+    903, 1001, 601, 902, 504, 602, 603, 505, 700, 1002, 506, 701, 507, 604, 605, 702, 800, 801, 703, 607, 704, 606,
+    802, 104, 803, 705, 707, 804, 105, 204, 706, 805, 807, 304, 205, 806, 106, 404, 305, 107, 904, 206, 508, 405,
+    509, 207, 306, 905, 510, 511, 608, 307, 609, 406, 906, 407, 611, 512, 907, 610, 513, 514, 708, 612, 709, 711,
+    614, 613, 515, 710, 808, 809, 811, 712, 615, 810, 714, 713, 812, 715, 813,
 )
 F32, BF16 = jnp.float32, jnp.bfloat16
 MESH_ID = pl.DeviceIdType.MESH
@@ -96,16 +96,18 @@
             src_ref=src, dst_ref=dst, device_id=peer, device_id_type=MESH_ID, **sems(j, stage)
         ).start()
 
+    def z_done(ref, j, stage):
+        return pltpu.make_async_remote_copy(
+            src_ref=ref, dst_ref=ref, device_id=other, device_id_type=MESH_ID, **sems(j, stage)
+        )
+
     def done(j, stage):
         r = pl.ds(0, sub)
         ref = (
-            lambda: zr1.at[j, pl.ds(0, NY * NC - 1)], lambda: zr2.at[j, pl.ds(0, NZL - 1)],
-            lambda: zg.at[j, pl.ds(0, NY - 1)], lambda: passed.at[j], lambda: yr.at[j], lambda: hr.at[j],
+            lambda: passed.at[j], lambda: yr.at[j], lambda: hr.at[j],
             lambda: out.at[0, pl.ds(0, 2), r], lambda: out.at[0, 0, r],
-        )[stage]()
-        return pltpu.make_async_remote_copy(
-            src_ref=ref, dst_ref=ref, device_id=other, device_id_type=MESH_ID, **sems(j, stage)
-        )
+        )[stage - 3]()
+        return z_done(ref, j, stage)
 
     def arrived(j, stage):
         got.add((j, stage))
@@ -127,10 +129,17 @@
 
     def z_send(j, value):
         zsend[j] = value.reshape(NY, part, rows)
-        zr1[j, me] = zsend[j, y]
-        for dy, dc in near:
-            peer = near_id(dy, dc)
-            send(zsend.at[j, peer["y"]], zr1.at[j, me], j, 0, peer)
+        for dy in (1, 2, 3):
+            to = lax.rem(y + dy, NY)
+            send(zsend.at[j, to], zr1.at[j, me], j, 0, {"y": to, "core": 1})
+
+        @pl.when(core == 0)
+        def _():
+            send(zsend.at[j, y], zr1.at[j, me], j, 0, {"core": 1})
+
+        @pl.when(core == 1)
+        def _():
+            zr1[j, me] = zsend[j, y]
 
     def term(s, owner):
         return jnp.dot(
@@ -146,24 +155,50 @@
         z_send(j, zpart[s] + term(s, across["x"]))
 
     def t2(j):
-        arrived(j, 0)
-        total = zr1[j, 0]
-        for i in range(1, NY * NC):
-            total += zr1[j, i]
-        zs2[j] = total
-        zr2[j, zl] = total
-        for dz in (1, 2, 3):
-            send(zs2.at[j], zr2.at[j, zl], j, 1, zl_id(dz))
+        @pl.when(core == 1)
+        def _():
+            z_done(zr1.at[j, pl.ds(0, NY * NC - 1)], j, 0).wait_recv()
+            total = zr1[j, 0]
+            for i in range(1, NY * NC):
+                total += zr1[j, i]
+            zs2[j] = total
+            zr2[j, zl] = total
+            for dz in (1, 2, 3):
+                send(zs2.at[j], zr2.at[j, zl], j, 1, zl_id(dz))
 
     def t3(j):
-        arrived(j, 1)
-        total = zr2[j, 0]
-        for i in range(1, NZL):
-            total += zr2[j, i]
-        factor = 1.0 if j < STREAMS else 1.0 / stretch
-        zg[j, y] = (total * factor).astype(BF16).astype(F32)
-        for dy in (1, 2, 3):
-            send(zg.at[j, y], zg.at[j, y], j, 2, y_id(dy))
+        @pl.when(core == 1)
+        def _():
+            z_done(zr2.at[j, pl.ds(0, NZL - 1)], j, 1).wait_recv()
+            total = zr2[j, 0]
+            for i in range(1, NZL):
+                total += zr2[j, i]
+            factor = 1.0 if j < STREAMS else 1.0 / stretch
+            zg[j, y] = (total * factor).astype(BF16).astype(F32)
+            for dy in (1, 2, 3):
+                for to in (0, 1):
+                    send(zg.at[j, y], zg.at[j, y], j, 2, {**y_id(dy), "core": to})
+            send(zg.at[j, y], zg.at[j, y], j, 2, {"core": 0})
+
+    def z_ready(j):
+        @pl.when(core == 0)
+        def _():
+            z_done(zg.at[j], j, 2).wait_recv()
+
+        @pl.when(core == 1)
+        def _():
+            z_done(zg.at[j, pl.ds(0, NY - 1)], j, 2).wait_recv()
+
+    def z_sent(j):
+        @pl.when(core == 0)
+        def _():
+            z_done(zr1.at[j, pl.ds(0, NY)], j, 0).wait_send()
+
+        @pl.when(core == 1)
+        def _():
+            z_done(zr1.at[j, pl.ds(0, NY - 1)], j, 0).wait_send()
+            z_done(zr2.at[j, pl.ds(0, NZL - 1)], j, 1).wait_send()
+            z_done(zr1.at[j, pl.ds(0, NY * NC - 1)], j, 2).wait_send()
 
     def block(j, owner):
         z = zg[j].reshape(depth, rows).astype(BF16)
@@ -176,7 +211,7 @@
         return [(j * PARTS + h, slice(h * sub, (h + 1) * sub)) for h in range(PARTS)]
 
     def t4(j):
-        arrived(j, 2)
+        z_ready(j)
         value = block(j, across["x"]).astype(BF16)
         for i, r in pieces(j):
             far[i, 0] = value[r, :half]
@@ -272,10 +307,13 @@
         kind, j = divmod(task, 100)
         tasks[kind](j)
     for j, stage in sent:
-        if (j, stage) not in got:
+        if stage >= 3 and (j, stage) not in got:
             arrived(j, stage)
+    for j in range(ITERS * STREAMS):
+        z_sent(j)
     for j, stage in sent:
-        done(j, stage).wait_send()
+        if stage >= 3:
+            done(j, stage).wait_send()
 
 
 def turn(blocks, out, turned, sems):

time: 110 us -> 106 us (0.964)
  Pallas kernels: 110 us -> 105 us
    pallas_call x1, Pallas kernels: 107 us -> 103 us  [body(): pl.pallas_call(functools.partial(kernel, math.sqrt(n_total / m_total)), o...]
where the time goes in v4:
time: 106 us; the launch traced here: 105 us
  Pallas kernels  105 us (99%)
    pallas_call x1, Pallas kernels, body(): pl.pallas_call(functools.partial(kernel, math.sqrt(n_total / m_total)), o...  103 us
    pallas_call x1, Pallas kernels, body(): pl.pallas_call(turn, out_shape=jax.ShapeDtypeStruct((ITERS, width, probe)...  2.26 us

profile of v4, /device:TPU:32, one launch (start us, length us, event | category | flops | bytes accessed | tf_op | source)
XLA Modules:
  0.0 105.0 jit_solution(15040531519886263689)
XLA Ops:
  0.0 102.5 %shard_map.28.blocks = bf16[2,4,128,2048]{3,2,1,0:T(8,128)(2,1)S(1)} custom-call(bf16[384,8192]{1,0:T(8,128)(2,1)} %a_hbm.1, bf16[8192,128]{1,0:T(8,128)(2,1)} %p_hbm.1), custom_call_target="tpu_custom_call" | custom-call | tf_op jit(solution)/shard_map/pallas_call | solution.py:341
  102.5 2.3 %shard_map.29 = bf16[2,8192,128]{2,1,0:T(8,128)(2,1)} custom-call(bf16[2,4,128,2048]{3,2,1,0:T(8,128)(2,1)S(1)} %shard_map.28.blocks), custom_call_target="tpu_custom_call" | custom-call | tf_op jit(solution)/shard_map/pallas_call | solution.py:375
